TPU v7x, 32 devices: a whole 2x2x4 slice. The times are simulated.
32 devices in a mesh: cells: 8 (over z, y), members: 4 (over x, core).
Axes of the slice: x: 2, y: 2, z: 4, core: 2. Of those that a mesh axis runs over, the one named last changes fastest.
Arguments:
- tmax: float32 [16, 97, 32768], P('members', None, 'cells'), may hold values from -24 to 24
- threshold: int32 [32768], P('cells'), may hold values from 0 to 79
- land_mask: int32 [32768], P('cells'), may hold values from 0 to 1, as said below
- region_id: int32 [32768], P('cells'), may hold values from 0 to 45, as said below
- block_fill: int32 [256], P('cells'), may hold values from 64 to 128
- cell_area: float32 [32768], P('cells'), may hold values from 0.1 to 1
Outputs:
- region_index: float32 [16, 92, 46], P('members')
- cell_mean: float32 [92, 32768], P('members', 'cells')
- land_count: int32 [46], replicated
Inputs may be any that keep to these rules, and one draw needn't show every extreme that they name: `land_mask`: in every block of 128 slots the first 46 slots are land. `region_id`: in every block of 128 slots the first 46 slots name every region once.
All inputs are finite; a program needn't handle non-finite values.
Results may differ from a plain program's by a relative error of at most 0.0003.
Values sent between devices are 32-bit elements; how exact they have to be, the bound alone decides.
A program may use at most 64 MiB of HBM per device.

v0:
```python
import jax
import jax.numpy as jnp
from jax import lax
from jax.sharding import PartitionSpec as P

WINDOW = 6
REGIONS = 46


def shards(tmax, threshold, land_mask, region_id, block_fill, cell_area):
    blocks = block_fill.shape[0]
    cell_dev = threshold.shape[0]
    slots = cell_dev // blocks
    position = lax.broadcasted_iota(jnp.int32, (blocks, slots), 1)
    inside = (position < block_fill[:, None]).astype(jnp.int32).reshape(cell_dev)
    live = land_mask * inside
    livef = live.astype(jnp.float32)
    weight = cell_area * livef
    matches = region_id[:, None] == jnp.arange(REGIONS, dtype=jnp.int32)[None, :]
    onehot = matches.astype(jnp.float32)
    area_part = jnp.dot(weight, onehot, precision=lax.Precision.HIGHEST)
    count_part = jnp.dot(livef, onehot, precision=lax.Precision.HIGHEST)
    limit = threshold.astype(jnp.float32) * 0.1
    members_here = tmax.shape[0]
    days = tmax.shape[1] - WINDOW + 1
    excess = jnp.maximum(tmax - limit[None, None, :], 0.0)
    rolled = excess[:, 0:days]
    for shift in range(1, WINDOW):
        rolled = rolled + excess[:, shift : shift + days]
    rolled = rolled / WINDOW
    weighted = (rolled * weight[None, None, :]).reshape(members_here * days, cell_dev)
    partial_value = jnp.dot(weighted, onehot, precision=lax.Precision.HIGHEST).reshape(
        members_here, days, REGIONS
    )
    area_sum, counted = lax.psum((area_part, count_part), "cells")
    sums = lax.psum(partial_value, "cells")
    region_index = sums / area_sum[None, None, :]
    land_count = counted.astype(jnp.int32)
    ensemble = lax.axis_size("members") * members_here
    member_part = jnp.sum(rolled, axis=0) * livef[None, :] / ensemble
    cell_mean = lax.psum_scatter(member_part, "members", scatter_dimension=0, tiled=True)
    return (region_index, cell_mean, land_count)


def solution(mesh):
    return jax.shard_map(
        shards,
        mesh=mesh,
        in_specs=(
            P("members", None, "cells"),
            P("cells"),
            P("cells"),
            P("cells"),
            P("cells"),
            P("cells"),
        ),
        out_specs=(P("members", None, None), P("members", "cells"), P()),
        check_vma=False,
    )
```

profile of v0, /device:TPU:0, one launch (start us, length us, event | category | flops | bytes accessed | tf_op | source)
XLA Modules:
  0.0 116.5 jit_solution(4286990216037394844)
XLA Ops:
  7.2 0.0 all-reduce.5.cloned.1.call-start
  7.2 0.7 convert_multiply_fusion
  7.9 4.5 %subtract_maximum_fusion = f32[4,97,4096]{2,0,1:T(4,128)S(1)} fusion(f32[4,97,4096]{2,0,1:T(4,128)} %param.6, f32[4096]{0:T(1024)S(1)} %convert_multiply_fusion), kind=kLoop, calls=%fused_computation | loop fusion | flops 3178496 | bytes 12730368 | tf_op jit(solution)/shard_map/max | solution.py:26
  12.4 0.0 copy-start.1
  12.4 0.0 copy-start.2
  12.4 0.0 copy-start.3
  12.4 12.3 %multiply_reduce_fusion = (f32[92,4096]{1,0:T(8,128)S(1)}, f32[4,92,4096]{2,0,1:T(4,128)S(1)}) fusion(f32[4,97,4096]{2,0,1:T(4,128)S(1)} %subtract_maximum_fusion), kind=kLoop, calls=%fused_computation.8 | loop fusion | flops 10174464 | bytes 43712512 | tf_op jit(solution)/shard_map/reduce_sum | solution.py:40
  24.8 0.0 copy-done.1
  24.8 0.0 copy-done.2
  24.8 0.0 copy-done.3
  24.8 0.1 broadcast_multiply_fusion.1
  24.9 0.0 copy-start
  24.9 2.4 %broadcast_multiply_fusion = f32[4,92,4096]{2,0,1:T(4,128)S(1)} fusion(f32[4,92,4096]{2,0,1:T(4,128)S(1)} %get-tuple-element.12, f32[4096]{0:T(1024)S(1)} %get-tuple-element.13), kind=kLoop, calls=%fused_computation.9 | loop fusion | flops 1507328 | bytes 12075008 | tf_op jit(solution)/shard_map/mul | solution.py:31
  27.3 0.0 copy-done
  27.3 0.0 copy-start.4
  27.4 7.5 %fusion.1 = f32[4,92,46]{1,2,0:T(8,128)} fusion(f32[4,92,4096]{2,0,1:T(4,128)S(1)} %broadcast_multiply_fusion, s32[4096]{0:T(1024)S(1)} %copy-done), kind=kOutput, calls=%fused_computation.1 | convolution fusion | flops 832233472 | bytes 6113408 | tf_op jit(solution)/shard_map/dot_general | solution.py:32
  34.9 0.0 all-reduce.5.cloned.1.call-update
  34.9 0.1 multiply_multiply_fusion
  35.1 20.1 %fusion = f32[24,4096]{1,0:T(8,128)S(1)} fusion(f32[92,4096]{1,0:T(8,128)S(1)} %multiply_multiply_fusion), kind=kCustom, calls=%all-reduce-scatter | all-reduce-scatter fusion | flops 393217 | bytes 1901056
  55.2 1.3 %collective-permute-start = (f32[3,4096]{1,0:T(4,128)S(1)}, f32[3,4096]{1,0:T(4,128)S(1)}, u32[]{:S(2)}, u32[]{:S(2)}) collective-permute-start(f32[3,4096]{1,0:T(4,128)S(1)} %slice.30), channel_id=1, source_target_pairs={{0,1},{1,2},{2,3},{4,5},{5,6},{6,7},{8,9},{9,10},{10,11},{12,13},{... | collective-permute-start | bytes 147464
  56.5 0.5 convolution_bitcast_fusion.1
  56.9 0.5 convolution_bitcast_fusion
  57.4 21.7 %all-reduce.2 = (f32[46]{0:T(128)S(1)}, f32[46]{0:T(128)S(1)}) all-reduce(f32[46]{0:T(128)S(1)} %convolution_bitcast_fusion.1, f32[46]{0:T(128)S(1)} %convolution_bitcast_fusion), channel_id=1, replica_groups=mesh['cells'=8,'members'=4] {'cells'}, use_global_device_ids=true, to_apply=%region_1.0 | all-reduce | flops 92 | bytes 736 | tf_op jit(solution)/shard_map/psum | solution.py:35
  79.1 0.5 convert_element_type.14
  79.6 0.0 copy-done.4
  79.6 0.6 dynamic-slice.4
  80.8 0.0 collective-permute-done
  80.8 0.4 concatenate
  81.2 0.8 constant_dynamic-slice_fusion
  82.0 26.0 %all-reduce.5.cloned.1.call-done = f32[4,92,46]{1,2,0:T(8,128)} async-done(((f32[4,92,46]{1,2,0:T(8,128)}), f32[4,92,46]{1,2,0:T(8,128)}) %all-reduce.5.cloned.1.call-update) | async-done | bytes 67728 | tf_op jit(solution)/shard_map/psum | solution.py:36
  108.0 1.0 broadcast_divide_fusion
  109.0 0.7 copy.12
  (1 shorter events, 0.0 us)
Async XLA Ops:
  7.2 100.8 %all-reduce.5.cloned.1.call-start = ((), (), s32[]{:S(2)}) async-start(), calls=%async_computation | async-start | bytes 196608 | tf_op jit(solution)/shard_map/psum | solution.py:36
  12.4 12.4 %copy-start.1 = (f32[4096]{0:T(1024)S(1)}, f32[4096]{0:T(1024)}, u32[]{:S(2)}) copy-start(f32[4096]{0:T(1024)} %param.11) | copy-start | bytes 49156
  12.4 12.4 %copy-start.2 = (s32[4096]{0:T(1024)S(1)}, s32[4096]{0:T(1024)}, u32[]{:S(2)}) copy-start(s32[4096]{0:T(1024)} %param.8) | copy-start | bytes 49156
  12.4 12.4 %copy-start.3 = (s32[32]{0:T(128)S(1)}, s32[32]{0:T(128)}, u32[]{:S(2)}) copy-start(s32[32]{0:T(128)} %param.10) | copy-start | bytes 388
  24.9 2.4 %copy-start = (s32[4096]{0:T(1024)S(1)}, s32[4096]{0:T(1024)}, u32[]{:S(2)}) copy-start(s32[4096]{0:T(1024)} %param.9) | copy-start | bytes 49156
  27.3 52.2 %copy-start.4 = (u32[32]{0:T(128)S(1)}, u32[32]{0:T(128)}, u32[]{:S(2)}) copy-start(u32[32]{0:T(128)} %constant.15) | copy-start | bytes 388
  55.2 25.7 %collective-permute-start = (f32[3,4096]{1,0:T(4,128)S(1)}, f32[3,4096]{1,0:T(4,128)S(1)}, u32[]{:S(2)}, u32[]{:S(2)}) collective-permute-start(f32[3,4096]{1,0:T(4,128)S(1)} %slice.30), channel_id=1, source_target_pairs={{0,1},{1,2},{2,3},{4,5},{5,6},{6,7},{8,9},{9,10},{10,11},{12,13},{... | collective-permute-start | bytes 147464
Sparse Core Ops, SparseCore 0:
  35.0 72.8 all-reduce.4
where the time goes:
time: 117 us; the launch traced here: 116 us
  blocking collectives  41.7 us (36%)
  waiting for transfers between devices  26 us (22%)
  other arithmetic  21.7 us (19%)
  between operations  14.8 us (13%)
  matrix products  8.47 us (7%)
  local copies, waits for them, and re-layouts  2.48 us (2%)
  starting transfers between devices  1.33 us (1%)
    psum x1, waiting for transfers between devices, shards(): sums = lax.psum(partial_value, 'cells')  26 us
    psum x1, blocking collectives, shards(): area_sum, counted = lax.psum((area_part, count_part), 'cells')  21.7 us
    unnamed x1, blocking collectives  20.1 us
    reduce_sum x1, other arithmetic, shards(): member_part = jnp.sum(rolled, axis=0) * livef[None, :] / ensemble  12.3 us
    dot_general x1, matrix products, shards(): jnp.dot(weighted, onehot, precision=lax.Precision.HIGHEST)  7.54 us
    max x1, other arithmetic, shards(): excess = jnp.maximum(tmax - limit[None, None, :], 0.0)  4.45 us
    mul x2, other arithmetic, shards(): rolled * weight[None, None, :]  2.51 us
    unnamed x15, local copies, waits for them, and re-layouts  2.48 us
  transfers between devices with their start and end apart: 2, of which 1 were waited for; matrix products, arithmetic and copies ran while one was open for 20% of the time, Pallas kernels for 0%

commit v1 on v0

v1 whole, which is shorter than its diff:
```python
import functools

import jax
import jax.numpy as jnp
from jax import lax
from jax.experimental import pallas as pl
from jax.experimental.pallas import tpu as pltpu
from jax.sharding import PartitionSpec as P

WINDOW = 6
REGIONS = 46
LANES = 128
TILES = 4
LAG = 3
QUARTERS = 4
MESH = pl.DeviceIdType.MESH


def up(n, step):
    return -(-n // step) * step


def kernel(
    dims,
    tmax_ref, thr_ref, land_ref, rid_ref, fill_ref, area_ref,
    region_ref, mean_ref, count_ref,
    x_buf, lhs, lhs_w, onehot, acc, acc_w, live_buf, s_buf, parts, got1, send2, got2,
    ep, rs_src, rs_got, mid_src, mid_got, whole,
    hbm_sem, s1_send, s1_recv, s2_send, s2_recv,
    rs_send, rs_recv, mid_send, mid_recv, ag_send, ag_recv,
):
    (members_here, in_days, days, chunks, width, slots, slot_rows, rows_out,
     pairs, share_rows, shares, groups, ensemble) = dims
    me_c = lax.axis_index("cells")
    me_m = lax.axis_index("members")
    group, mine = lax.div(me_c, shares), lax.rem(me_c, shares)
    side, core = lax.div(me_m, 2), lax.rem(me_m, 2)
    partner = side * 2 + (1 - core)
    across = (1 - side) * 2 + core

    def share_peer(k):
        return group * shares + lax.rem(mine + k, shares)

    def group_peer(k):
        return lax.rem(group + k, groups) * shares + mine

    barrier = pltpu.get_barrier_semaphore()
    for m in (partner, across):
        pl.semaphore_signal(barrier, inc=1, device_id={"members": m}, device_id_type=MESH)
    for k in range(1, shares):
        pl.semaphore_signal(barrier, inc=1, device_id={"cells": share_peer(k)}, device_id_type=MESH)
    for k in range(1, groups):
        pl.semaphore_signal(barrier, inc=1, device_id={"cells": group_peer(k)}, device_id_type=MESH)

    def load(c):
        return pltpu.make_async_copy(
            tmax_ref.at[:, :, pl.ds(c * width, width)], x_buf.at[c], hbm_sem.at[c]
        )

    for c in range(chunks):
        load(c).start()

    def copy1(c):
        return pltpu.make_async_remote_copy(
            src_ref=parts.at[c, 1 - core], dst_ref=got1.at[c],
            send_sem=s1_send.at[c], recv_sem=s1_recv.at[c],
            device_id={"members": partner}, device_id_type=MESH,
        )

    def copy2(c):
        return pltpu.make_async_remote_copy(
            src_ref=send2.at[c], dst_ref=got2.at[c],
            send_sem=s2_send.at[c], recv_sem=s2_recv.at[c],
            device_id={"members": across}, device_id_type=MESH,
        )

    region_rows = up(REGIONS, 16)
    onehot[...] = jnp.zeros_like(onehot)
    lhs[...] = jnp.zeros_like(lhs)
    acc[...] = jnp.zeros_like(acc)
    acc_w[...] = jnp.zeros_like(acc_w)
    ep[...] = jnp.zeros_like(ep)

    contract = (((1,), (1,)), ((), ()))

    def compute(c):
        at = pl.ds(pl.multiple_of(c * width, width), width)
        lane = lax.broadcasted_iota(jnp.int32, (1, LANES), 1)
        inside = jnp.concatenate(
            [(lane < fill_ref[c * TILES + j]).astype(jnp.int32) for j in range(TILES)], axis=1
        )
        live = (land_ref[:, at] * inside).astype(jnp.float32)
        live_buf[c] = live
        weight = area_ref[:, at] * live
        limit = thr_ref[:, at].astype(jnp.float32) * 0.1
        names = lax.broadcasted_iota(jnp.int32, (region_rows, width), 0)
        hot = jnp.where(names == rid_ref[:, at], 1.0, 0.0)
        onehot[0:region_rows, :] = hot.astype(jnp.bfloat16)
        line = lax.broadcasted_iota(jnp.int32, (16, width), 0)
        w_high = weight.astype(jnp.bfloat16).astype(jnp.float32)
        lhs_w[...] = jnp.where(
            line == 0, w_high,
            jnp.where(line == 1, weight - w_high, jnp.where(line == 2, live, 0.0)),
        ).astype(jnp.bfloat16)
        load(c).wait()
        total = None
        for m in range(members_here):
            excess = jnp.maximum(x_buf[c, m] - limit, 0.0)
            total = excess if total is None else total + excess
            weighted = excess * weight
            high = weighted.astype(jnp.bfloat16)
            low = (weighted - high.astype(jnp.float32)).astype(jnp.bfloat16)
            lhs[m, 0:in_days, :] = high
            lhs[m, slot_rows : slot_rows + in_days, :] = low
            acc[m] += lax.dot_general(
                lhs[m], onehot[...], contract, preferred_element_type=jnp.float32
            )
        s_buf[...] = total
        for d in range(4):
            lo = d * rows_out
            two = s_buf[lo : lo + rows_out + 4] + s_buf[lo + 1 : lo + rows_out + 5]
            parts[c, d % 2, d // 2] = two[0:rows_out] + two[2 : rows_out + 2] + two[4 : rows_out + 4]
        acc_w[...] += lax.dot_general(
            lhs_w[...], onehot[...], contract, preferred_element_type=jnp.float32
        )

    def cross(c):
        copy1(c).wait_recv()
        send2[c] = parts[c, core, 1 - side] + got1[c, 1 - side]
        copy2(c).start()

    compute(0)
    pl.semaphore_wait(barrier, 2 + (shares - 1) + (groups - 1))
    copy1(0).start()

    def step(c, carry):
        compute(c)
        copy1(c).start()

        @pl.when(c >= LAG)
        def _():
            cross(c - LAG)

        return carry

    lax.fori_loop(1, chunks, step, 0)

    def of_member(m):
        return acc[m, 0:in_days] + acc[m, slot_rows : slot_rows + in_days]

    for p in range(pairs):
        ep[p, 0:in_days] = of_member(2 * p) + pltpu.roll(of_member(2 * p + 1), LANES // 2, 1)
    area_row = acc_w[0:1] + acc_w[1:2]
    count_row = acc_w[2:3]
    line = lax.broadcasted_iota(jnp.int32, (share_rows, LANES), 0)
    for p in range(pairs):
        for q in range(QUARTERS):
            lo = q * share_rows
            rolled = ep[p, lo : lo + share_rows]
            for k in range(1, WINDOW):
                rolled = rolled + ep[p, lo + k : lo + k + share_rows]
            rolled = rolled / WINDOW
            for row, value in ((days, area_row), (days + 1, count_row)):
                if lo <= row < lo + share_rows:
                    rolled = jnp.where(line == row - lo, value, rolled)
            rs_src[p * QUARTERS + q] = rolled

    def rs_copy(k):
        return pltpu.make_async_remote_copy(
            src_ref=rs_src.at[lax.rem(mine + k, shares)], dst_ref=rs_got.at[k - 1],
            send_sem=rs_send.at[k - 1], recv_sem=rs_recv.at[k - 1],
            device_id={"cells": share_peer(k)}, device_id_type=MESH,
        )

    def mid_copy(k):
        return pltpu.make_async_remote_copy(
            src_ref=mid_src, dst_ref=mid_got.at[k - 1],
            send_sem=mid_send.at[k - 1], recv_sem=mid_recv.at[k - 1],
            device_id={"cells": group_peer(k)}, device_id_type=MESH,
        )

    def ag_copy(k):
        return pltpu.make_async_remote_copy(
            src_ref=whole.at[mine], dst_ref=whole.at[mine],
            send_sem=ag_send.at[k - 1], recv_sem=ag_recv.at[k - 1],
            device_id={"cells": share_peer(k)}, device_id_type=MESH,
        )

    for k in range(1, shares):
        rs_copy(k).start()
    for c in range(max(chunks - LAG, 0), chunks):
        cross(c)
    own = rs_src[mine]
    for k in range(1, shares):
        rs_copy(k).wait_recv()
        own = own + rs_got[k - 1]
    if groups > 1:
        mid_src[...] = own
        for k in range(1, groups):
            mid_copy(k).start()
        for k in range(1, groups):
            mid_copy(k).wait_recv()
            own = own + mid_got[k - 1]
    whole[mine] = own
    for k in range(1, shares):
        ag_copy(k).start()

    def finish(c):
        copy2(c).wait_recv()
        at = slice(c * width, (c + 1) * width)
        total = parts[c, core, side] + got1[c, side] + got2[c]
        mean_ref[:, at] = total * live_buf[c] / (WINDOW * ensemble)

    late = chunks - 2
    for c in range(late):
        finish(c)
    for k in range(1, shares):
        ag_copy(k).wait_recv()
    all_shares = whole[...]
    spot = lambda row: all_shares[row // share_rows, row % share_rows : row % share_rows + 1]
    area = spot(days)
    count_ref[...] = spot(days + 1)[:, 0:REGIONS].astype(jnp.int32)
    for p in range(pairs):
        sums = all_shares[p * QUARTERS : (p + 1) * QUARTERS].reshape(QUARTERS * share_rows, LANES)
        region_ref[2 * p] = sums[0:days, 0:REGIONS] / area[:, 0:REGIONS]
        sums = pltpu.roll(sums, LANES // 2, 1)
        region_ref[2 * p + 1] = sums[0:days, 0:REGIONS] / area[:, 0:REGIONS]
    for c in range(late, chunks):
        finish(c)
    for c in range(chunks):
        copy1(c).wait_send()
        copy2(c).wait_send()
    for k in range(1, shares):
        rs_copy(k).wait_send()
        ag_copy(k).wait_send()
    for k in range(1, groups):
        mid_copy(k).wait_send()


def shards(n_cells, n_members, tmax, threshold, land_mask, region_id, block_fill, cell_area):
    members_here, in_days, cell_dev = tmax.shape
    days = in_days - WINDOW + 1
    slots = cell_dev // block_fill.shape[0]
    assert slots == LANES and n_members == 4 and members_here % 2 == 0
    width = TILES * slots
    chunks = cell_dev // width
    slot_rows = up(in_days, 16)
    rows_out = days // n_members
    pairs = members_here // 2
    share_rows = up(-(-(days + 2) // QUARTERS), 8)
    shares = pairs * QUARTERS
    groups = n_cells // shares
    ensemble = n_members * members_here
    dims = (members_here, in_days, days, chunks, width, slots, slot_rows, rows_out,
            pairs, share_rows, shares, groups, ensemble)
    f32, bf16 = jnp.float32, jnp.bfloat16
    dma = pltpu.SemaphoreType.DMA
    vmem = pl.BlockSpec(memory_space=pltpu.VMEM)
    others = max(groups - 1, 1)
    ep_rows = up(QUARTERS * share_rows + WINDOW - 1, 8)
    row = lambda v: v.reshape(1, cell_dev)
    region, mean, count = pl.pallas_call(
        functools.partial(kernel, dims),
        name="warm_spell",
        out_shape=(
            jax.ShapeDtypeStruct((members_here, days, REGIONS), f32),
            jax.ShapeDtypeStruct((rows_out, cell_dev), f32),
            jax.ShapeDtypeStruct((1, REGIONS), jnp.int32),
        ),
        in_specs=[
            pl.BlockSpec(memory_space=pl.ANY), vmem, vmem, vmem,
            pl.BlockSpec(memory_space=pltpu.SMEM), vmem,
        ],
        out_specs=(vmem, vmem, vmem),
        scratch_shapes=[
            pltpu.VMEM((chunks, members_here, in_days, width), f32),
            pltpu.VMEM((members_here, 2 * slot_rows, width), bf16),
            pltpu.VMEM((16, width), bf16),
            pltpu.VMEM((LANES, width), bf16),
            pltpu.VMEM((members_here, 2 * slot_rows, LANES), f32),
            pltpu.VMEM((16, LANES), f32),
            pltpu.VMEM((chunks, 1, width), f32),
            pltpu.VMEM((in_days, width), f32),
            pltpu.VMEM((chunks, 2, 2, rows_out, width), f32),
            pltpu.VMEM((chunks, 2, rows_out, width), f32),
            pltpu.VMEM((chunks, rows_out, width), f32),
            pltpu.VMEM((chunks, rows_out, width), f32),
            pltpu.VMEM((pairs, ep_rows, LANES), f32),
            pltpu.VMEM((shares, share_rows, LANES), f32),
            pltpu.VMEM((shares - 1, share_rows, LANES), f32),
            pltpu.VMEM((share_rows, LANES), f32),
            pltpu.VMEM((others, share_rows, LANES), f32),
            pltpu.VMEM((shares, share_rows, LANES), f32),
            dma((chunks,)), dma((chunks,)), dma((chunks,)), dma((chunks,)), dma((chunks,)),
            dma((shares - 1,)), dma((shares - 1,)), dma((others,)), dma((others,)),
            dma((shares - 1,)), dma((shares - 1,)),
        ],
        compiler_params=pltpu.CompilerParams(
            collective_id=0, has_side_effects=True, vmem_limit_bytes=48 * 1024 * 1024
        ),
    )(tmax, row(threshold), row(land_mask), row(region_id), block_fill, row(cell_area))
    return region, mean, count.reshape(REGIONS)


def solution(mesh):
    body = functools.partial(shards, mesh.shape["cells"], mesh.shape["members"])
    return jax.shard_map(
        body,
        mesh=mesh,
        in_specs=(
            P("members", None, "cells"),
            P("cells"),
            P("cells"),
            P("cells"),
            P("cells"),
            P("cells"),
        ),
        out_specs=(P("members", None, None), P("members", "cells"), P()),
        check_vma=False,
    )
```

time: 117 us -> 32.6 us (0.28)
  blocking collectives: 41.7 us -> 0 us
  waiting for transfers between devices: 26 us -> 0 us
  other arithmetic: 21.7 us -> 0 us
  Pallas kernels: 0 us -> 20.4 us
  between operations: 14.8 us -> 0.7 us
  local copies, waits for them, and re-layouts: 2.48 us -> 11.4 us
  matrix products: 8.47 us -> 0 us
  starting transfers between devices: 1.33 us -> 0 us
    psum x1 -> x0, waiting for transfers between devices: 26 us -> none  [shards(): sums = lax.psum(partial_value, 'cells')]
    psum x1 -> x0, blocking collectives: 21.7 us -> none  [shards(): area_sum, counted = lax.psum((area_part, count_part), 'cells')]
    pallas_call x0 -> x1, Pallas kernels: none -> 20.4 us  [shards(): pl.pallas_call(functools.partial(kernel, dims), name='warm_spell', out_sh...]
    unnamed x1 -> x0, blocking collectives: 20.1 us -> none
    reduce_sum x1 -> x0, other arithmetic: 12.3 us -> none  [shards(): member_part = jnp.sum(rolled, axis=0) * livef[None, :] / ensemble]
    unnamed x15 -> x14, local copies, waits for them, and re-layouts: 2.48 us -> 11.4 us
    dot_general x3 -> x0, matrix products: 8.47 us -> none  [the longest x1 7.54 us: shards(): jnp.dot(weighted, onehot, precision=lax.Precision.HIGHEST)]
    max x1 -> x0, other arithmetic: 4.45 us -> none  [shards(): excess = jnp.maximum(tmax - limit[None, None, :], 0.0)]
  transfers between devices with their start and end apart: 2 -> 0, of which waited for: 1 -> 0; matrix products, arithmetic and copies ran while one was open for 20% -> 0% of each run, Pallas kernels for 0% -> 0%
where the time goes in v1:
time: 32.6 us; the launch traced here: 32.4 us
  Pallas kernels  20.4 us (63%)
  local copies, waits for them, and re-layouts  11.4 us (35%)
  between operations  0.7 us (2%)
    pallas_call x1, Pallas kernels, shards(): pl.pallas_call(functools.partial(kernel, dims), name='warm_spell', out_sh...  20.4 us
    unnamed x14, local copies, waits for them, and re-layouts  11.4 us

profile of v1, /device:TPU:0, one launch (start us, length us, event | category | flops | bytes accessed | tf_op | source)
XLA Modules:
  0.0 32.4 jit_solution(3331552349228304021)
XLA Ops:
  0.6 0.0 copy-start.3
  0.6 0.0 copy-start.4
  0.7 0.0 copy-start.2
  0.7 0.0 copy-start.1
  0.7 0.0 copy-start
  0.7 9.3 %copy.9.tmax_ref = f32[4,97,4096]{2,1,0:T(8,128)} copy(f32[4,97,4096]{2,0,1:T(4,128)} %param.6) | data formatting | bytes 12713984 | tf_op args[0]
  10.0 0.0 copy-done.3
  10.0 0.0 copy-done.4
  10.0 0.0 copy-done.2
  10.0 0.0 copy-done.1
  10.0 0.0 copy-done
  10.0 20.4 %warm_spell.1 = (f32[4,92,46]{2,1,0:T(8,128)S(1)}, f32[23,4096]{1,0:T(8,128)S(1)}, s32[1,46]{1,0:T(1,128)S(1)}) custom-call(f32[4,97,4096]{2,1,0:T(8,128)} %copy.9.tmax_ref, s32[1,4096]{1,0:T(1,128)S(1)} %bitcast.5, s32[1,4096]{1,0:T(1,128)S(1)} %bitcast.6, s32[1,4096]{1,0:T(1,128)S(1)} %bitcast.7, s32[32]{0:T(128)S(1)} %copy-done.4, f32[1,4096]{1,0:T(1,128)S(1)} %bitcast.8), custom_call_target="tpu_custom_call" | custom-call | tf_op jit(solution)/shard_map/warm_spell/pallas_call | solution.py:262
  30.4 0.8 %copy.10 = f32[4,92,46]{1,0,2:T(4,128)} copy(f32[4,92,46]{2,1,0:T(8,128)S(1)} %get-tuple-element.9) | data formatting | bytes 135424
  31.1 0.7 %copy.13 = f32[23,4096]{1,0:T(8,128)} copy(f32[23,4096]{1,0:T(8,128)S(1)} %get-tuple-element.16) | data formatting | bytes 753664
  31.9 0.5 %copy.14 = s32[46]{0:T(128)} copy(s32[46]{0:T(128)S(1)} %bitcast.9) | data formatting | bytes 368
Async XLA Ops:
  0.6 9.4 %copy-start.3 = (f32[4096]{0:T(1024)S(1)}, f32[4096]{0:T(1024)}, u32[]{:S(2)}) copy-start(f32[4096]{0:T(1024)} %param.11) | copy-start | bytes 49156
  0.6 9.4 %copy-start.4 = (s32[32]{0:T(128)S(1)}, s32[32]{0:T(128)}, u32[]{:S(2)}) copy-start(s32[32]{0:T(128)} %fill_ref.1) | copy-start | bytes 388
  0.7 9.3 %copy-start.2 = (s32[4096]{0:T(1024)S(1)}, s32[4096]{0:T(1024)}, u32[]{:S(2)}) copy-start(s32[4096]{0:T(1024)} %param.9) | copy-start | bytes 49156
  0.7 9.3 %copy-start.1 = (s32[4096]{0:T(1024)S(1)}, s32[4096]{0:T(1024)}, u32[]{:S(2)}) copy-start(s32[4096]{0:T(1024)} %param.8) | copy-start | bytes 49156
  0.7 9.3 %copy-start = (s32[4096]{0:T(1024)S(1)}, s32[4096]{0:T(1024)}, u32[]{:S(2)}) copy-start(s32[4096]{0:T(1024)} %param.7) | copy-start | bytes 49156

commit v2 on v1

--- a/solution.py
+++ b/solution.py
@@ -52,9 +52,22 @@
     for k in range(1, groups):
         pl.semaphore_signal(barrier, inc=1, device_id={"cells": group_peer(k)}, device_id_type=MESH)
 
+    rows = TILES * members_here
+    in_rows = x_buf.shape[1]
+    x_flat = x_buf.reshape(chunks * in_rows * rows, LANES)
+
+    def days_of(c, m):
+        return jnp.concatenate(
+            [
+                x_flat[pl.ds(c * (in_rows * rows) + j * members_here + m, in_rows, stride=rows), :]
+                for j in range(TILES)
+            ],
+            axis=1,
+        )
+
     def load(c):
         return pltpu.make_async_copy(
-            tmax_ref.at[:, :, pl.ds(c * width, width)], x_buf.at[c], hbm_sem.at[c]
+            tmax_ref.at[:, pl.ds(c * rows, rows), :], x_buf.at[c, pl.ds(0, in_days)], hbm_sem.at[c]
         )
 
     for c in range(chunks):
@@ -105,13 +118,13 @@
         load(c).wait()
         total = None
         for m in range(members_here):
-            excess = jnp.maximum(x_buf[c, m] - limit, 0.0)
+            excess = jnp.maximum(days_of(c, m) - limit, 0.0)
             total = excess if total is None else total + excess
             weighted = excess * weight
             high = weighted.astype(jnp.bfloat16)
             low = (weighted - high.astype(jnp.float32)).astype(jnp.bfloat16)
-            lhs[m, 0:in_days, :] = high
-            lhs[m, slot_rows : slot_rows + in_days, :] = low
+            lhs[m, 0:in_rows, :] = high
+            lhs[m, slot_rows : slot_rows + in_rows, :] = low
             acc[m] += lax.dot_general(
                 lhs[m], onehot[...], contract, preferred_element_type=jnp.float32
             )
@@ -244,7 +257,7 @@
     assert slots == LANES and n_members == 4 and members_here % 2 == 0
     width = TILES * slots
     chunks = cell_dev // width
-    slot_rows = up(in_days, 16)
+    slot_rows, in_rows = up(in_days, 16), up(in_days, 8)
     rows_out = days // n_members
     pairs = members_here // 2
     share_rows = up(-(-(days + 2) // QUARTERS), 8)
@@ -258,6 +271,9 @@
     vmem = pl.BlockSpec(memory_space=pltpu.VMEM)
     others = max(groups - 1, 1)
     ep_rows = up(QUARTERS * share_rows + WINDOW - 1, 8)
+    tiles = cell_dev // LANES
+    view = tmax.transpose(1, 0, 2).reshape(in_days, members_here, tiles, LANES)
+    view = view.transpose(0, 2, 1, 3).reshape(in_days, tiles * members_here, LANES)
     row = lambda v: v.reshape(1, cell_dev)
     region, mean, count = pl.pallas_call(
         functools.partial(kernel, dims),
@@ -273,14 +289,14 @@
         ],
         out_specs=(vmem, vmem, vmem),
         scratch_shapes=[
-            pltpu.VMEM((chunks, members_here, in_days, width), f32),
+            pltpu.VMEM((chunks, in_rows, TILES * members_here, LANES), f32),
             pltpu.VMEM((members_here, 2 * slot_rows, width), bf16),
             pltpu.VMEM((16, width), bf16),
             pltpu.VMEM((LANES, width), bf16),
             pltpu.VMEM((members_here, 2 * slot_rows, LANES), f32),
             pltpu.VMEM((16, LANES), f32),
             pltpu.VMEM((chunks, 1, width), f32),
-            pltpu.VMEM((in_days, width), f32),
+            pltpu.VMEM((in_rows, width), f32),
             pltpu.VMEM((chunks, 2, 2, rows_out, width), f32),
             pltpu.VMEM((chunks, 2, rows_out, width), f32),
             pltpu.VMEM((chunks, rows_out, width), f32),
@@ -298,7 +314,7 @@
         compiler_params=pltpu.CompilerParams(
             collective_id=0, has_side_effects=True, vmem_limit_bytes=48 * 1024 * 1024
         ),
-    )(tmax, row(threshold), row(land_mask), row(region_id), block_fill, row(cell_area))
+    )(view, row(threshold), row(land_mask), row(region_id), block_fill, row(cell_area))
     return region, mean, count.reshape(REGIONS)
 
 

time: 32.6 us -> 27.8 us (0.85)
  local copies, waits for them, and re-layouts: 11.4 us -> 5.54 us
  Pallas kernels: 20.4 us -> 21.1 us
    unnamed x14 -> x13, local copies, waits for them, and re-layouts: 11.4 us -> 5.54 us
    pallas_call x1, Pallas kernels: 20.4 us -> 21.1 us  [shards(): pl.pallas_call(functools.partial(kernel, dims), name='warm_spell', out_sh...]
where the time goes in v2:
time: 27.8 us; the launch traced here: 27.3 us
  Pallas kernels  21.1 us (76%)
  local copies, waits for them, and re-layouts  5.54 us (20%)
  between operations  0.65 us (2%)
    pallas_call x1, Pallas kernels, shards(): pl.pallas_call(functools.partial(kernel, dims), name='warm_spell', out_sh...  21.1 us
    unnamed x13, local copies, waits for them, and re-layouts  5.54 us

profile of v2, /device:TPU:0, one launch (start us, length us, event | category | flops | bytes accessed | tf_op | source)
XLA Modules:
  0.0 27.3 jit_solution(9127211257948773147)
XLA Ops:
  0.6 0.0 copy-start
  0.6 0.7 %copy-done = s32[4096]{0:T(1024)S(1)} copy-done((s32[4096]{0:T(1024)S(1)}, s32[4096]{0:T(1024)}, u32[]{:S(2)}) %copy-start) | copy-done | bytes 16408
  1.4 0.0 copy-start.1
  1.4 0.7 %copy-done.1 = s32[4096]{0:T(1024)S(1)} copy-done((s32[4096]{0:T(1024)S(1)}, s32[4096]{0:T(1024)}, u32[]{:S(2)}) %copy-start.1) | copy-done | bytes 16408
  2.1 0.0 copy-start.2
  2.1 0.7 %copy-done.2 = s32[4096]{0:T(1024)S(1)} copy-done((s32[4096]{0:T(1024)S(1)}, s32[4096]{0:T(1024)}, u32[]{:S(2)}) %copy-start.2) | copy-done | bytes 16408
  2.8 0.0 copy-start.3
  2.8 0.7 %copy-done.3 = f32[4096]{0:T(1024)S(1)} copy-done((f32[4096]{0:T(1024)S(1)}, f32[4096]{0:T(1024)}, u32[]{:S(2)}) %copy-start.3) | copy-done | bytes 16408
  3.5 0.0 copy-start.4
  3.5 0.7 %copy-done.4 = s32[32]{0:T(128)S(1)} copy-done((s32[32]{0:T(128)S(1)}, s32[32]{0:T(128)}, u32[]{:S(2)}) %copy-start.4) | copy-done | bytes 152
  4.2 21.1 %warm_spell.1 = (f32[4,92,46]{2,1,0:T(8,128)S(1)}, f32[23,4096]{1,0:T(8,128)S(1)}, s32[1,46]{1,0:T(1,128)S(1)}) custom-call(f32[97,128,128]{2,1,0:T(8,128)} %bitcast.17, s32[1,4096]{1,0:T(1,128)S(1)} %bitcast.12, s32[1,4096]{1,0:T(1,128)S(1)} %bitcast.13, s32[1,4096]{1,0:T(1,128)S(1)} %bitcast.14, s32[32]{0:T(128)S(1)} %copy-done.4, f32[1,4096]{1,0:T(1,128)S(1)} %bitcast.15), custom_call_target="tpu_custom_call" | custom-call | tf_op jit(solution)/shard_map/warm_spell/pallas_call | solution.py:278
  25.3 0.8 %copy.10 = f32[4,92,46]{1,0,2:T(4,128)} copy(f32[4,92,46]{2,1,0:T(8,128)S(1)} %get-tuple-element.9) | data formatting | bytes 135424
  26.0 0.7 %copy.13 = f32[23,4096]{1,0:T(8,128)} copy(f32[23,4096]{1,0:T(8,128)S(1)} %get-tuple-element.16) | data formatting | bytes 753664
  26.8 0.5 %copy.14 = s32[46]{0:T(128)} copy(s32[46]{0:T(128)S(1)} %bitcast.16) | data formatting | bytes 368
Async XLA Ops:
  0.6 0.7 %copy-start = (s32[4096]{0:T(1024)S(1)}, s32[4096]{0:T(1024)}, u32[]{:S(2)}) copy-start(s32[4096]{0:T(1024)} %param.7) | copy-start | bytes 49156
  1.4 0.7 %copy-start.1 = (s32[4096]{0:T(1024)S(1)}, s32[4096]{0:T(1024)}, u32[]{:S(2)}) copy-start(s32[4096]{0:T(1024)} %param.8) | copy-start | bytes 49156
  2.1 0.7 %copy-start.2 = (s32[4096]{0:T(1024)S(1)}, s32[4096]{0:T(1024)}, u32[]{:S(2)}) copy-start(s32[4096]{0:T(1024)} %param.9) | copy-start | bytes 49156
  2.8 0.7 %copy-start.3 = (f32[4096]{0:T(1024)S(1)}, f32[4096]{0:T(1024)}, u32[]{:S(2)}) copy-start(f32[4096]{0:T(1024)} %param.11) | copy-start | bytes 49156
  3.5 0.7 %copy-start.4 = (s32[32]{0:T(128)S(1)}, s32[32]{0:T(128)}, u32[]{:S(2)}) copy-start(s32[32]{0:T(128)} %fill_ref.1) | copy-start | bytes 388

commit v3 on v2

--- a/solution.py
+++ b/solution.py
@@ -22,11 +22,11 @@
 
 def kernel(
     dims,
-    tmax_ref, thr_ref, land_ref, rid_ref, fill_ref, area_ref,
+    tmax_ref, thr_hbm, land_hbm, rid_hbm, fill_hbm, area_hbm,
     region_ref, mean_ref, count_ref,
-    x_buf, lhs, lhs_w, onehot, acc, acc_w, live_buf, s_buf, parts, got1, send2, got2,
+    thr_ref, land_ref, rid_ref, fill_ref, area_ref, x_buf, lhs, lhs_w, onehot, acc, acc_w, live_buf, s_buf, parts, got1, send2, got2,
     ep, rs_src, rs_got, mid_src, mid_got, whole,
-    hbm_sem, s1_send, s1_recv, s2_send, s2_recv,
+    small_sem, hbm_sem, s1_send, s1_recv, s2_send, s2_recv,
     rs_send, rs_recv, mid_send, mid_recv, ag_send, ag_recv,
 ):
     (members_here, in_days, days, chunks, width, slots, slot_rows, rows_out,
@@ -44,6 +44,15 @@
     def group_peer(k):
         return lax.rem(group + k, groups) * shares + mine
 
+    small = [
+        pltpu.make_async_copy(src, dst, small_sem.at[n])
+        for n, (src, dst) in enumerate((
+            (rid_hbm, rid_ref), (fill_hbm, fill_ref), (land_hbm, land_ref),
+            (area_hbm, area_ref), (thr_hbm, thr_ref),
+        ))
+    ]
+    for copy in small:
+        copy.start()
     barrier = pltpu.get_barrier_semaphore()
     for m in (partner, across):
         pl.semaphore_signal(barrier, inc=1, device_id={"members": m}, device_id_type=MESH)
@@ -70,8 +79,8 @@
             tmax_ref.at[:, pl.ds(c * rows, rows), :], x_buf.at[c, pl.ds(0, in_days)], hbm_sem.at[c]
         )
 
-    for c in range(chunks):
-        load(c).start()
+    load(0).start()
+    load(1).start()
 
     def copy1(c):
         return pltpu.make_async_remote_copy(
@@ -142,6 +151,10 @@
         send2[c] = parts[c, core, 1 - side] + got1[c, 1 - side]
         copy2(c).start()
 
+    for c in range(2, chunks):
+        load(c).start()
+    for copy in small:
+        copy.wait()
     compute(0)
     pl.semaphore_wait(barrier, 2 + (shares - 1) + (groups - 1))
     copy1(0).start()
@@ -284,11 +297,15 @@
             jax.ShapeDtypeStruct((1, REGIONS), jnp.int32),
         ),
         in_specs=[
-            pl.BlockSpec(memory_space=pl.ANY), vmem, vmem, vmem,
-            pl.BlockSpec(memory_space=pltpu.SMEM), vmem,
+            pl.BlockSpec(memory_space=pltpu.HBM) for _ in range(6)
         ],
         out_specs=(vmem, vmem, vmem),
         scratch_shapes=[
+            pltpu.VMEM((1, cell_dev), jnp.int32),
+            pltpu.VMEM((1, cell_dev), jnp.int32),
+            pltpu.VMEM((1, cell_dev), jnp.int32),
+            pltpu.SMEM(block_fill.shape, jnp.int32),
+            pltpu.VMEM((1, cell_dev), f32),
             pltpu.VMEM((chunks, in_rows, TILES * members_here, LANES), f32),
             pltpu.VMEM((members_here, 2 * slot_rows, width), bf16),
             pltpu.VMEM((16, width), bf16),
@@ -307,12 +324,12 @@
             pltpu.VMEM((share_rows, LANES), f32),
             pltpu.VMEM((others, share_rows, LANES), f32),
             pltpu.VMEM((shares, share_rows, LANES), f32),
-            dma((chunks,)), dma((chunks,)), dma((chunks,)), dma((chunks,)), dma((chunks,)),
+            dma((5,)), dma((chunks,)), dma((chunks,)), dma((chunks,)), dma((chunks,)), dma((chunks,)),
             dma((shares - 1,)), dma((shares - 1,)), dma((others,)), dma((others,)),
             dma((shares - 1,)), dma((shares - 1,)),
         ],
         compiler_params=pltpu.CompilerParams(
-            collective_id=0, has_side_effects=True, vmem_limit_bytes=48 * 1024 * 1024
+            collective_id=0, has_side_effects=True, vmem_limit_bytes=67043328
         ),
     )(view, row(threshold), row(land_mask), row(region_id), block_fill, row(cell_area))
     return region, mean, count.reshape(REGIONS)

time: 27.8 us -> 27 us (0.971)
  local copies, waits for them, and re-layouts: 5.54 us -> 4.63 us
  Pallas kernels: 21.1 us -> 21.5 us
    unnamed x13 -> x3, local copies, waits for them, and re-layouts: 5.54 us -> 4.63 us
    pallas_call x1, Pallas kernels: 21.1 us -> 21.5 us  [shards(): pl.pallas_call(functools.partial(kernel, dims), name='warm_spell', out_sh...]
where the time goes in v3:
time: 27 us; the launch traced here: 26.7 us
  Pallas kernels  21.5 us (80%)
  local copies, waits for them, and re-layouts  4.63 us (17%)
  between operations  0.64 us (2%)
    pallas_call x1, Pallas kernels, shards(): pl.pallas_call(functools.partial(kernel, dims), name='warm_spell', out_sh...  21.5 us
    unnamed x3, local copies, waits for them, and re-layouts  4.63 us

profile of v3, /device:TPU:0, one launch (start us, length us, event | category | flops | bytes accessed | tf_op | source)
XLA Modules:
  0.0 26.7 jit_solution(6591129423070852030)
XLA Ops:
  0.6 21.5 %warm_spell.1 = (f32[4,92,46]{2,1,0:T(8,128)}, f32[23,4096]{1,0:T(8,128)}, s32[1,46]{1,0:T(1,128)}) custom-call(f32[97,128,128]{2,1,0:T(8,128)} %bitcast.12, s32[1,4096]{1,0:T(1,128)} %bitcast.13, s32[1,4096]{1,0:T(1,128)} %bitcast.14, s32[1,4096]{1,0:T(1,128)} %bitcast.15, s32[32]{0:T(128)} %fill_hbm.1, f32[1,4096]{1,0:T(1,128)} %bitcast.16), custom_call_target="tpu_custom_call" | custom-call | tf_op jit(solution)/shard_map/warm_spell/pallas_call | solution.py:291
  22.1 1.7 %copy.10 = f32[4,92,46]{1,0,2:T(4,128)} copy(f32[4,92,46]{2,1,0:T(8,128)} %get-tuple-element.9) | data formatting | bytes 135424
  23.8 1.8 %copy.13 = f32[23,4096]{1,0:T(8,128)} copy(f32[23,4096]{1,0:T(8,128)} %get-tuple-element.16) | data formatting | bytes 753664
  25.6 1.2 %copy.14 = s32[46]{0:T(128)} copy(s32[46]{0:T(128)} %bitcast.17) | data formatting | bytes 368
